TPU v7x, 256 devices: a whole 4x4x8 slice. The times are simulated.
256 devices in a mesh: seq: 16 (over x, y), head: 16 (over z, core).
Axes of the slice: x: 4, y: 4, z: 8, core: 2. Of those that a mesh axis runs over, the one named last changes fastest.
Arguments:
- video_rows: bfloat16 [8192, 5120], P('seq'), may hold values from -6 to 6
- context: bfloat16 [512, 5120], P('seq'), may hold values from -6 to 6
- valid_length: int32 [1], replicated, may hold values from 64 to 512
- timestep: int32 [1], replicated, may hold values from 0 to 999
- query_weight: bfloat16 [5120, 4096], P('seq', 'head'), may hold values from -0.078125 to 0.078125
- key_weight: bfloat16 [5120, 4096], P('seq', 'head'), may hold values from -0.078125 to 0.078125
- value_weight: bfloat16 [5120, 4096], P('seq', 'head'), may hold values from -0.078125 to 0.078125
- out_weight: bfloat16 [4096, 5120], P('head', 'seq'), may hold values from -0.09375 to 0.09375
- query_gain: float32 [4096], P('head'), may hold values from 0.5 to 15
- key_gain: float32 [4096], P('head'), may hold values from 0.5 to 15
- time_weight: bfloat16 [2, 256, 5120], P(None, None, 'head'), may hold values from -0.375 to 0.375
- modulation: float32 [2, 5120], P(None, 'head'), may hold values from -3 to 3
Outputs:
- residual_out: bfloat16 [8192, 5120], P('seq', 'head')
- modulated: bfloat16 [8192, 5120], P('seq', 'head')
Inputs may be any that keep to these rules, and one draw needn't show every extreme that they name: `valid_length`: text positions at or beyond it are padding.
All inputs are finite; a program needn't handle non-finite values.
Results may differ from a plain program's by a relative error of at most 0.0065.
The roundings to bfloat16 on the way count: a program that leaves them out, or rounds other values in their place, can miss the bound.
Values may be sent and summed in bfloat16 or wider, within the bound.
A program may use at most 64 MiB of HBM per device.

v0:
```python
import jax
import jax.numpy as jnp
from jax import lax
from jax.sharding import Mesh
from jax.sharding import PartitionSpec as P

HD = 128
FREQ = 256
SEQ = ("seq_0", "seq_1")


def joined_along(parts, dim):
    parts = jnp.moveaxis(parts, 0, dim)
    lengths = parts.shape
    return parts.reshape(*lengths[:dim], lengths[dim] * lengths[dim + 1], *lengths[dim + 2 :])


def from_everyone(shard, axis):
    copies = jnp.broadcast_to(shard, (lax.axis_size(axis), *shard.shape))
    return lax.all_to_all(copies, axis, split_axis=0, concat_axis=0, tiled=True)


def gathered_copies(shard, axis, dim):
    return joined_along(from_everyone(shard, axis), dim)


def side_by_side(arrays, axis, dim, along):
    ends, at = ([], 0)
    for a in arrays[:-1]:
        at += a.shape[along]
        ends.append(at)
    both = jnp.concatenate(arrays, axis=along)
    return tuple(jnp.split(lax.all_gather(both, axis, axis=dim, tiled=True), ends, axis=along))


def of_everyone(shard, axis):
    everything = from_everyone(shard, axis)
    return jnp.sum(everything, axis=0)


def in_one(arrays, axis):
    ends = [0]
    for a in arrays:
        ends.append(ends[-1] + a.size)
    so_far = of_everyone(jnp.concatenate([a.ravel() for a in arrays]), axis)
    return tuple((so_far[b:e].reshape(a.shape) for a, b, e in zip(arrays, ends, ends[1:])))


def gathered_by_axis(shard, axes, dim):
    if not axes:
        return shard
    nearer = lax.all_gather(shard, axes[-1], axis=dim, tiled=True)
    return gathered_by_axis(nearer, axes[:-1], dim)


def layer_norm(rows):
    mean = jnp.mean(rows, axis=-1, keepdims=True)
    spread = jnp.mean((rows - mean) ** 2, axis=-1, keepdims=True)
    return (rows - mean) / jnp.sqrt(spread + 1e-06)


def add_rows(left, piece):
    return jnp.dot(left, piece, preferred_element_type=jnp.float32)


def project_pair(source, key_weight):
    empty = jnp.zeros((source.shape[0], key_weight.shape[1]), jnp.float32)

    def add_both(totals, pieces, start):
        return (add_rows(source, pieces[0]), add_rows(source, pieces[1]))

    return (empty, add_both)


def on_device(
    video_rows,
    context,
    valid_length,
    timestep,
    query_weight,
    key_weight,
    value_weight,
    out_weight,
    query_gain,
    key_gain,
    time_weight,
    modulation,
):
    tok_rows = video_rows.shape[0]
    local_att = query_weight.shape[1]
    width_local = modulation.shape[1]
    heads_local = local_att // HD
    normed = layer_norm(video_rows.astype(jnp.float32)).astype(jnp.bfloat16)
    queries = add_rows(normed, gathered_copies(query_weight, SEQ, 0))
    empty, add_both = project_pair(context, key_weight)
    key_proj, value_full = add_both(
        (empty, empty), side_by_side((key_weight, value_weight), SEQ, 0, 1), jnp.int32(0)
    )
    query_sq, key_sq = in_one(
        (jnp.sum(queries * queries, axis=1), jnp.sum(key_proj * key_proj, axis=1)), "head"
    )
    total_att = local_att * lax.axis_size("head")
    query_normed = (queries / jnp.sqrt(query_sq[:, None] / total_att + 1e-06) * query_gain).astype(
        jnp.bfloat16
    )
    key_normed = (key_proj / jnp.sqrt(key_sq[:, None] / total_att + 1e-06) * key_gain).astype(
        jnp.bfloat16
    )
    value_proj = value_full.astype(jnp.bfloat16)
    key_normed, value_proj = side_by_side((key_normed, value_proj), SEQ, 0, 1)
    text_count = key_normed.shape[0]
    key_valid = jnp.arange(text_count, dtype=jnp.int32) < valid_length[0]
    query_heads = query_normed.reshape(tok_rows, heads_local, HD)
    key_heads = key_normed.reshape(text_count, heads_local, HD)
    value_heads = value_proj.reshape(text_count, heads_local, HD)
    scores = jnp.einsum(
        "thd,shd->hts", query_heads, key_heads, preferred_element_type=jnp.float32
    ) * HD ** (-0.5)
    scores = jnp.where(key_valid[None, None, :], scores, jnp.float32(-1e30))
    shifted = jnp.exp(scores - jnp.max(scores, axis=-1, keepdims=True))
    weights = (shifted / jnp.sum(shifted, axis=-1, keepdims=True)).astype(jnp.bfloat16)
    attended = jnp.einsum(
        "hts,shd->thd", weights, value_heads, preferred_element_type=jnp.float32
    ).astype(jnp.bfloat16)
    attended = attended.reshape(tok_rows, local_att)
    terms = jnp.dot(
        attended, gathered_by_axis(out_weight, SEQ, 1), preferred_element_type=jnp.float32
    )
    projected = lax.psum_scatter(terms, "head", scatter_dimension=1, tiled=True)
    video_part = lax.dynamic_slice_in_dim(
        video_rows, lax.axis_index("head") * width_local, width_local, 1
    )
    residual_out = (video_part.astype(jnp.float32) + projected).astype(jnp.bfloat16)
    half = FREQ // 2
    freqs = jnp.exp(-jnp.log(10000.0) * jnp.arange(half, dtype=jnp.float32) / half)
    angles = timestep[0].astype(jnp.float32) * freqs
    embedding = jnp.concatenate([jnp.cos(angles), jnp.sin(angles)])
    act = jax.nn.silu(embedding).astype(jnp.bfloat16)[None, :]
    shift = modulation[0] + jnp.dot(act, time_weight[0], preferred_element_type=jnp.float32)[0]
    scale = modulation[1] + jnp.dot(act, time_weight[1], preferred_element_type=jnp.float32)[0]
    resid = residual_out.astype(jnp.float32)
    row_sum, row_squares = in_one((jnp.sum(resid, axis=1), jnp.sum(resid * resid, axis=1)), "head")
    full_width = width_local * lax.axis_size("head")
    mean2 = (row_sum / full_width)[:, None]
    var2 = (row_squares / full_width)[:, None] - mean2 * mean2
    modulated = ((resid - mean2) / jnp.sqrt(var2 + 1e-06) * (1.0 + scale) + shift).astype(
        jnp.bfloat16
    )
    return (residual_out, modulated)


def solution(mesh):
    split = Mesh(mesh.devices.reshape(4, 4, mesh.shape["head"]), ("seq_0", "seq_1", "head"))
    return jax.shard_map(
        on_device,
        mesh=split,
        in_specs=(
            P(SEQ, None),
            P(SEQ, None),
            P(),
            P(),
            P(SEQ, "head"),
            P(SEQ, "head"),
            P(SEQ, "head"),
            P("head", SEQ),
            P("head"),
            P("head"),
            P(None, None, "head"),
            P(None, "head"),
        ),
        out_specs=(P(SEQ, "head"), P(SEQ, "head")),
        check_vma=False,
    )
```

profile of v0, /device:TPU:1, one launch (start us, length us, event | category | flops | bytes accessed | tf_op | source)
XLA Modules:
  0.0 244.4 jit_solution(14297226721645430427)
XLA Ops:
  7.2 0.0 copy-start
  7.2 0.0 all-gather.3.cloned.1.call-start
  7.2 1.8 pad_maximum_fusion
  9.0 0.0 all-gather.3.cloned.1.call-update
  9.0 2.7 %broadcast_in_dim.18 = bf16[16,320,256]{2,1,0:T(8,128)(2,1)} broadcast(bf16[320,256]{1,0:T(8,128)(2,1)} %param.16), dimensions={1,2} | broadcast | bytes 2785280 | tf_op jit(solution)/shard_map/broadcast_in_dim | solution.py:19
  11.7 0.0 copy-start.2
  11.7 7.7 %all-to-all-start = ((bf16[16,320,256]{2,1,0:T(8,128)(2,1)}), bf16[16,320,256]{2,1,0:T(8,128)(2,1)S(1)}, u32[]{:S(2)}, u32[]{:S(2)}) async-start(bf16[16,320,256]{2,1,0:T(8,128)(2,1)} %broadcast_in_dim.18), calls=%async_computation | async-start | bytes 5242880 | tf_op jit(solution)/shard_map/all_to_all | solution.py:20
  19.4 0.0 all-gather.5.cloned.1.call-start
  19.5 0.0 copy-done.2
  19.5 40.4 %all_gather.14 = bf16[256,1280]{0,1:T(8,128)(2,1)} all-gather(bf16[256,320]{0,1:T(8,128)(2,1)S(1)} %copy-done.2), channel_id=1, replica_groups=mesh['seq_0'=4,'seq_1'=4,'head'=16] {'seq_1'}, dimensions={1}, use_global_device_ids=true | all-gather | bytes 819200 | tf_op jit(solution)/shard_map/all_gather | solution.py:52
  59.9 0.0 all-gather.5.cloned.1.call-update
  60.6 3.3 %convert_reduce_fusion = f32[512]{0:T(512)S(1)} fusion(bf16[512,5120]{1,0:T(8,128)(2,1)} %param.12), kind=kLoop, calls=%fused_computation.2 | loop fusion | flops 5242368 | bytes 5244928 | tf_op jit(solution)/shard_map/reduce_sum | solution.py:57
  63.8 4.0 %fusion.3 = f32[512]{0:T(512)S(1)} fusion(bf16[512,5120]{1,0:T(8,128)(2,1)} %param.12, f32[512]{0:T(512)S(1)} %broadcast_multiply_fusion), kind=kLoop, calls=%fused_computation.5 | loop fusion | flops 10485248 | bytes 5246976 | tf_op jit(solution)/shard_map/reduce_sum | solution.py:58
  67.8 0.0 all-to-all-done
  67.8 4.5 %multiply_reduce_fusion = (f32[512]{0:T(512)S(1)}, f32[512,256]{0,1:T(8,128)S(1)}) fusion(bf16[5120,256]{1,0:T(8,128)(2,1)S(1)} %bitcast.46, bf16[512,5120]{1,0:T(8,128)(2,1)} %param.12, f32[512]{0:T(512)S(1)} %add_sqrt_fusion.2, f32[512]{0:T(512)S(1)} %broadcast_multiply_fusion), kind=kOutput, calls=%fused_computation.37 | convolution fusion | flops 1352924672 | bytes 8394752 | tf_op jit(solution)/shard_map/dot_general | solution.py:63
  72.3 0.0 copy-start.6
  72.4 24.8 %all-gather.3.cloned.1.call-done = bf16[5120,512]{1,0:T(8,128)(2,1)} async-done(((bf16[320,512]{1,0:T(8,128)(2,1)}), bf16[5120,512]{1,0:T(8,128)(2,1)}) %all-gather.3.cloned.1.call-update) | async-done | bytes 5242896 | tf_op jit(solution)/shard_map/all_gather | solution.py:33
  97.1 0.0 copy-done
  97.1 2.4 multiply_reduce_fusion.1
  99.6 0.6 broadcast_in_dim.19
  100.2 7.9 %all-to-all-start.1 = ((f32[16,1,544]{2,1,0:T(1,128)}), f32[16,1,544]{2,1,0:T(1,128)S(1)}, u32[]{:S(2)}, u32[]{:S(2)}) async-start(f32[16,1,544]{2,1,0:T(1,128)} %broadcast_in_dim.19), calls=%async_computation.1 | async-start | bytes 81920 | tf_op jit(solution)/shard_map/all_to_all | solution.py:20
  108.1 0.0 copy-start.5
  108.1 0.0 reduce-scatter.2.cloned.1.call-start
  108.1 2.3 fusion.15
  110.4 5.1 %all-to-all-done.1 = f32[16,1,544]{2,1,0:T(1,128)S(1)} async-done(((f32[16,1,544]{2,1,0:T(1,128)}), f32[16,1,544]{2,1,0:T(1,128)S(1)}, u32[]{:S(2)}, u32[]{:S(2)}) %all-to-all-start.1) | async-done | bytes 34848 | tf_op jit(solution)/shard_map/all_to_all | solution.py:20
  115.5 0.0 copy-done.6
  115.6 0.1 fusion.44
  115.7 22.4 %all_gather.13 = bf16[512,512]{1,0:T(8,128)(2,1)S(1)} all-gather(bf16[32,512]{1,0:T(8,128)(2,1)S(1)} %pad_maximum_fusion.1), channel_id=1, replica_groups=mesh['seq_0'=4,'seq_1'=4,'head'=16] {'seq_0','seq_1'}, dimensions={0}, use_global_device_ids=true | all-gather | bytes 557056 | tf_op jit(solution)/shard_map/all_gather | solution.py:33
  138.1 0.1 copy.33
  138.3 0.0 copy-done.5
  138.3 0.1 multiply_convert_fusion
  138.4 0.8 fusion.57
  139.3 1.1 convolution_convert_fusion
  140.3 0.0 all-gather.5.cloned.1.call-done
  140.4 7.2 %fusion.60 = f32[512,5120]{0,1:T(8,128)} fusion(bf16[256,5120]{0,1:T(8,128)(2,1)} %all-gather.5.cloned.1.call-done, bf16[512,256]{0,1:T(8,128)(2,1)S(1)} %bitcast.47), kind=kOutput, calls=%fused_computation.73 | convolution fusion | flops 1342177280 | bytes 13369344 | tf_op jit(solution)/shard_map/dot_general | solution.py:126
  147.6 0.0 reduce-scatter.2.cloned.1.call-update
  147.6 0.0 copy-start.3
  147.6 0.0 copy-start.4
  147.7 1.3 constant_dynamic-slice_fusion
  148.9 0.2 copy.36
  149.9 68.9 %reduce-scatter.2.cloned.1.call-done = f32[512,320]{0,1:T(8,128)} async-done(((f32[512,5120]{0,1:T(8,128)}), f32[512,320]{0,1:T(8,128)}) %reduce-scatter.2.cloned.1.call-update) | async-done | bytes 655376 | tf_op jit(solution)/shard_map/reduce_scatter | solution.py:129
  218.7 1.2 convert_reduce_fusion.1
  220.0 0.0 copy-start.1
  220.0 0.7 broadcast_in_dim.22
  220.7 8.4 %all-to-all-start.2 = ((f32[16,1,1024]{2,1,0:T(1,128)}), f32[16,1,1024]{2,1,0:T(1,128)S(1)}, u32[]{:S(2)}, u32[]{:S(2)}) async-start(f32[16,1,1024]{2,1,0:T(1,128)} %broadcast_in_dim.22), calls=%async_computation.3 | async-start | bytes 131072 | tf_op jit(solution)/shard_map/all_to_all | solution.py:20
  229.1 0.0 copy-done.3
  229.1 0.0 copy-done.4
  229.1 0.2 fusion.18
  229.3 0.2 fusion.20
  229.5 7.4 %all-to-all-done.2 = f32[16,1,1024]{2,1,0:T(1,128)S(1)} async-done(((f32[16,1,1024]{2,1,0:T(1,128)}), f32[16,1,1024]{2,1,0:T(1,128)S(1)}, u32[]{:S(2)}, u32[]{:S(2)}) %all-to-all-start.2) | async-done | bytes 65568 | tf_op jit(solution)/shard_map/all_to_all | solution.py:20
  236.9 0.1 reduce_sum.89
  237.0 0.9 fusion.28
  237.8 0.0 copy-done.1
  (14 shorter events, 0.2 us)
Async XLA Ops:
  7.2 90.0 %copy-start = (bf16[32,5120]{1,0:T(8,128)(2,1)S(1)}, bf16[32,5120]{1,0:T(8,128)(2,1)}, u32[]{:S(2)}) copy-start(bf16[32,5120]{1,0:T(8,128)(2,1)} %param.13) | copy-start | bytes 983044
  7.2 90.0 %all-gather.3.cloned.1.call-start = ((), (), s32[]{:S(2)}) async-start(), calls=%async_computation.4 | async-start | bytes 5570560 | tf_op jit(solution)/shard_map/all_gather | solution.py:33
  11.7 7.8 %copy-start.2 = (bf16[256,320]{0,1:T(8,128)(2,1)S(1)}, bf16[256,320]{0,1:T(8,128)(2,1)}, u32[]{:S(2)}) copy-start(bf16[256,320]{0,1:T(8,128)(2,1)} %param.19) | copy-start | bytes 491524
  11.7 56.1 %all-to-all-start = ((bf16[16,320,256]{2,1,0:T(8,128)(2,1)}), bf16[16,320,256]{2,1,0:T(8,128)(2,1)S(1)}, u32[]{:S(2)}, u32[]{:S(2)}) async-start(bf16[16,320,256]{2,1,0:T(8,128)(2,1)} %broadcast_in_dim.18), calls=%async_computation | async-start | bytes 5242880 | tf_op jit(solution)/shard_map/all_to_all | solution.py:20
  19.4 120.9 %all-gather.5.cloned.1.call-start = ((), (), s32[]{:S(2)}) async-start(), calls=%async_computation.5 | async-start | bytes 3276800 | tf_op jit(solution)/shard_map/all_gather | solution.py:52
  72.3 43.2 %copy-start.6 = (f32[256]{0:T(256)S(1)}, f32[256]{0:T(256)}, u32[]{:S(2)}) copy-start(f32[256]{0:T(256)} %param.21) | copy-start | bytes 3076
  100.2 15.3 %all-to-all-start.1 = ((f32[16,1,544]{2,1,0:T(1,128)}), f32[16,1,544]{2,1,0:T(1,128)S(1)}, u32[]{:S(2)}, u32[]{:S(2)}) async-start(f32[16,1,544]{2,1,0:T(1,128)} %broadcast_in_dim.19), calls=%async_computation.1 | async-start | bytes 81920 | tf_op jit(solution)/shard_map/all_to_all | solution.py:20
  108.1 30.2 %copy-start.5 = (f32[256]{0:T(256)S(1)}, f32[256]{0:T(256)}, u32[]{:S(2)}) copy-start(f32[256]{0:T(256)} %param.20) | copy-start | bytes 3076
  108.1 110.6 %reduce-scatter.2.cloned.1.call-start = ((), (), s32[]{:S(2)}) async-start(), calls=%async_computation.6 | async-start | bytes 11141120 | tf_op jit(solution)/shard_map/reduce_scatter | solution.py:129
  147.6 81.5 %copy-start.3 = (bf16[2,256,320]{1,2,0:T(8,128)(2,1)S(1)}, bf16[2,256,320]{1,2,0:T(8,128)(2,1)}, u32[]{:S(2)}) copy-start(bf16[2,256,320]{1,2,0:T(8,128)(2,1)} %param.22) | copy-start | bytes 983044
  147.6 81.5 %copy-start.4 = (f32[2,320]{1,0:T(2,128)S(1)}, f32[2,320]{1,0:T(2,128)}, u32[]{:S(2)}) copy-start(f32[2,320]{1,0:T(2,128)} %param.23) | copy-start | bytes 7684
  220.0 17.9 %copy-start.1 = (bf16[512,320]{0,1:T(8,128)(2,1)}, bf16[512,320]{0,1:T(8,128)(2,1)S(1)}, u32[]{:S(2)}) copy-start(bf16[512,320]{0,1:T(8,128)(2,1)S(1)} %get-tuple-element.4) | copy-start | bytes 983044
  220.7 16.2 %all-to-all-start.2 = ((f32[16,1,1024]{2,1,0:T(1,128)}), f32[16,1,1024]{2,1,0:T(1,128)S(1)}, u32[]{:S(2)}, u32[]{:S(2)}) async-start(f32[16,1,1024]{2,1,0:T(1,128)} %broadcast_in_dim.22), calls=%async_computation.3 | async-start | bytes 131072 | tf_op jit(solution)/shard_map/all_to_all | solution.py:20
Sparse Core Ops, SparseCore 0:
  11.0 86.0 all-gather.2
  98.9 39.6 all-gather.4
  147.7 70.9 reduce-scatter.1
where the time goes:
time: 245 us; the launch traced here: 244 us
  waiting for transfers between devices  106 us (43%)
  blocking collectives  62.8 us (26%)
  starting transfers between devices  24.1 us (10%)
  matrix products  18.7 us (8%)
  between operations  15.3 us (6%)
  other arithmetic  11.6 us (5%)
  local copies, waits for them, and re-layouts  5.73 us (2%)
    reduce_scatter x1, waiting for transfers between devices, on_device(): projected = lax.psum_scatter(terms, 'head', scatter_dimension=1, tiled=True)  68.9 us
    all_gather x1, blocking collectives, gathered_by_axis(): nearer = lax.all_gather(shard, axes[-1], axis=dim, tiled=True)  40.4 us
    all_gather x1, waiting for transfers between devices, side_by_side(): lax.all_gather(both, axis, axis=dim, tiled=True)  24.8 us
    all_to_all x3, starting transfers between devices, from_everyone(): return lax.all_to_all(copies, axis, split_axis=0, concat_axis=0, tiled=True)  24 us
    all_gather x1, blocking collectives, side_by_side(): lax.all_gather(both, axis, axis=dim, tiled=True)  22.4 us
    all_to_all x3, waiting for transfers between devices, from_everyone(): return lax.all_to_all(copies, axis, split_axis=0, concat_axis=0, tiled=True)  12.4 us
    dot_general x3, matrix products, add_rows(): return jnp.dot(left, piece, preferred_element_type=jnp.float32)  9.18 us
    dot_general x1, matrix products, on_device(): jnp.dot(attended, gathered_by_axis(out_weight, SEQ, 1), preferred_element...  7.25 us
  transfers between devices with their start and end apart: 6, of which 4 were waited for; matrix products, arithmetic and copies ran while one was open for 10% of the time, Pallas kernels for 0%

commit v1 on v0

v1 whole, which is shorter than its diff:
```python
import functools

import jax
import jax.numpy as jnp
from jax import lax
from jax.experimental import pallas as pl
from jax.experimental.pallas import tpu as pltpu
from jax.sharding import Mesh
from jax.sharding import PartitionSpec as P

HD = 128
FREQ = 256
SEQ = ("x", "y")
DEV = pl.DeviceIdType.MESH
F32 = jnp.float32
BF16 = jnp.bfloat16


def remote(src, dst, send, recv, dev):
    return pltpu.make_async_remote_copy(
        src_ref=src, dst_ref=dst, send_sem=send, recv_sem=recv, device_id=dev, device_id_type=DEV
    )


class PlaneGather:
    def __init__(self, buf, send, recv, coords, a1, a2, r0, n):
        self.buf, self.send_sems, self.recv_sems = buf, send, recv
        self.a1, self.a2, self.p, self.q = a1, a2, coords[a1], coords[a2]
        self.whole, self.qa, self.qb = (r0, n), (r0, n // 2), (r0 + n // 2, n // 2)

    OFFS = (0, 3, 1, 2)

    def copy(self, idx, di, dq, rows, axis, step):
        i, j = lax.rem(self.p + di, 4), lax.rem(self.q + dq, 4)
        r = pl.ds(rows[0], rows[1])
        ref = self.buf.at[i, j, r] if self.a1 == "x" else self.buf.at[j, i, r]
        dev = {axis: lax.rem((self.p if axis == self.a1 else self.q) + step, 4)}
        return remote(ref, ref, self.send_sems.at[idx], self.recv_sems.at[idx], dev)

    def start(self):
        self.copy(0, 0, 0, self.whole, self.a1, 1).start()
        self.copy(1, 0, 0, self.whole, self.a1, 3).start()
        self.column(0)

    def column(self, i):
        self.copy(4 + 4 * i, self.OFFS[i], 0, self.whole, self.a2, 1).start()
        self.copy(5 + 4 * i, self.OFFS[i], 0, self.whole, self.a2, 3).start()

    def first(self):
        self.copy(0, 3, 0, self.whole, self.a1, 1).wait_recv()
        self.copy(2, 3, 0, self.qa, self.a1, 1).start()
        self.copy(1, 1, 0, self.whole, self.a1, 3).wait_recv()
        self.copy(3, 1, 0, self.qb, self.a1, 3).start()
        self.column(1)
        self.column(2)

    def pass_on(self, i):
        o = self.OFFS[i]
        self.copy(4 + 4 * i, o, 3, self.whole, self.a2, 1).wait_recv()
        self.copy(6 + 4 * i, o, 3, self.qa, self.a2, 1).start()
        self.copy(5 + 4 * i, o, 1, self.whole, self.a2, 3).wait_recv()
        self.copy(7 + 4 * i, o, 1, self.qb, self.a2, 3).start()

    def second(self):
        self.copy(2, 2, 0, self.qa, self.a1, 1).wait_recv()
        self.copy(3, 2, 0, self.qb, self.a1, 3).wait_recv()
        self.column(3)

    def finish(self):
        for i in range(4):
            o = self.OFFS[i]
            self.copy(6 + 4 * i, o, 2, self.qa, self.a2, 1).wait_recv()
            self.copy(7 + 4 * i, o, 2, self.qb, self.a2, 3).wait_recv()

    def wait_sends(self):
        self.copy(0, 0, 0, self.whole, self.a1, 1).wait_send()
        self.copy(1, 0, 0, self.whole, self.a1, 3).wait_send()
        self.copy(2, 3, 0, self.qa, self.a1, 1).wait_send()
        self.copy(3, 1, 0, self.qb, self.a1, 3).wait_send()
        for i in range(4):
            o = self.OFFS[i]
            self.copy(4 + 4 * i, o, 0, self.whole, self.a2, 1).wait_send()
            self.copy(5 + 4 * i, o, 0, self.whole, self.a2, 3).wait_send()
            self.copy(6 + 4 * i, o, 3, self.qa, self.a2, 1).wait_send()
            self.copy(7 + 4 * i, o, 1, self.qb, self.a2, 3).wait_send()


def diagonal(n):
    return lax.broadcasted_iota(jnp.int32, (n, n), 0) == lax.broadcasted_iota(jnp.int32, (n, n), 1)


def kernel(
    valid_ref, x_hbm, ctx_hbm, wq_hbm, wk_hbm, wv_hbm, wo_hbm, qg_ref, kg_ref,
    resid_ref, stat_ref,
    xv, nv, wq, wo, wo_own, ctxv, ctxs, ctxr, wkv, part, red, kv, vt, qt, att, acc, xt, gcol,
    ssk_own, ssk, ssq_own, ssq, st_own, st,
    load_sems, gq_s, gq_r, go_s, go_r, tp_s, tp_r, cx_s, cx_r, rd_s, rd_r, kv_s, kv_r,
    sk_s, sk_r, sq_s, sq_r, st_s, st_r, z_s, z_r, d_s, d_r,
):
    x, y, z, c = (lax.axis_index(a) for a in ("x", "y", "z", "c"))
    coords = {"x": x, "y": y}
    s, h = x * 4 + y, z * 2 + c
    tokens, width = xv.shape
    depth = width // 16
    heads = wq.shape[3]

    block = tokens // 8
    x_loads = [
        pltpu.make_async_copy(
            x_hbm.at[pl.ds(i * block, block)], xv.at[pl.ds(i * block, block)], load_sems.at[i]
        )
        for i in range(8)
    ]
    ctx_load = pltpu.make_async_copy(ctx_hbm, ctxv, load_sems.at[8])
    wq_load = pltpu.make_async_copy(wq_hbm, wq.at[x, y], load_sems.at[9])
    wk_load = pltpu.make_async_copy(
        wk_hbm, wkv.at[pl.ds(0, depth), pl.ds(0, heads)], load_sems.at[10]
    )
    wv_load = pltpu.make_async_copy(
        wv_hbm, wkv.at[pl.ds(0, depth), pl.ds(heads, heads)], load_sems.at[11]
    )
    wo_load = pltpu.make_async_copy(wo_hbm, wo_own, load_sems.at[12])
    ctx_load.start()
    wq_load.start()
    for load in x_loads:
        load.start()
    wk_load.start()
    wv_load.start()
    wo_load.start()

    barrier = pltpu.get_barrier_semaphore()

    def plane(k, sign=1):
        dx, dy = lax.div(k, 4), lax.rem(k, 4)
        if sign < 0:
            dx, dy = 4 - dx, 4 - dy
        return {"x": lax.rem(x + dx, 4), "y": lax.rem(y + dy, 4)}

    def line(k):
        return {"z": lax.rem(z + lax.div(k, 2), 8), "c": lax.rem(c + lax.rem(k, 2), 2)}

    partner = {"x": lax.div(h, 4), "y": lax.rem(h, 4), "z": lax.div(s, 2), "c": lax.rem(s, 2)}

    def each_peer(f):
        def step(k, carry):
            f(k)
            return carry

        lax.fori_loop(1, 16, step, 0)

    def greet(k):
        pl.semaphore_signal(barrier, inc=1, device_id=plane(k), device_id_type=DEV)
        pl.semaphore_signal(barrier, inc=1, device_id=line(k), device_id_type=DEV)

    each_peer(greet)

    @pl.when(s != h)
    def _():
        pl.semaphore_signal(barrier, inc=1, device_id=partner, device_id_type=DEV)

    def norm_rows(lo, hi):
        def step(i, carry):
            rows = pl.ds(pl.multiple_of(i * 16, 16), 16)
            v = xv[rows, :].astype(F32)
            mean = jnp.mean(v, axis=-1, keepdims=True)
            d = v - mean
            spread = jnp.mean(d * d, axis=-1, keepdims=True)
            nv[rows, :] = (d * (1.0 / jnp.sqrt(spread + 1e-06))).astype(BF16)
            return carry

        lax.fori_loop(lo // 16, hi // 16, step, 0)

    ctx_load.wait()
    for i in range(16):
        ctxs[i, :, 0:depth] = ctxv[:, i * depth : (i + 1) * depth]
        ctxs[i, :, depth:] = jnp.zeros((ctxs.shape[1], ctxs.shape[2] - depth), BF16)
    ctxr[0] = ctxs[s]
    wkv[depth:, :] = jnp.zeros((wkv.shape[0] - depth, wkv.shape[1]), BF16)
    wq_load.wait()
    x_loads[0].wait()
    x_loads[1].wait()
    norm_rows(0, 2 * block)

    @pl.when(s != h)
    def _():
        pl.semaphore_wait(barrier, 31)

    @pl.when(s == h)
    def _():
        pl.semaphore_wait(barrier, 30)

    def ctx_copy(k):
        dev = plane(k)
        return remote(
            ctxs.at[dev["x"] * 4 + dev["y"]], ctxr.at[k], cx_s.at[k], cx_r.at[k], dev
        )

    each_peer(lambda k: ctx_copy(k).start())

    half = wq.shape[2] // 2
    gq = [
        PlaneGather(wq, gq_s.at[0], gq_r.at[0], coords, "x", "y", 0, half),
        PlaneGather(wq, gq_s.at[1], gq_r.at[1], coords, "y", "x", half, half),
    ]
    for g in gq:
        g.start()

    x_loads[2].wait()
    norm_rows(2 * block, 3 * block)

    wk_load.wait()
    wv_load.wait()
    each_peer(lambda k: ctx_copy(k).wait_recv())
    rows = ctxr.shape[1]
    part[...] = jnp.dot(
        ctxr[...].reshape(16 * rows, ctxr.shape[2]), wkv[...], preferred_element_type=F32
    ).reshape(16, rows, 2 * heads)

    def red_copy(k):
        return remote(part.at[k], red.at[k], rd_s.at[k], rd_r.at[k], plane(k, -1))

    each_peer(lambda k: red_copy(k).start())
    for g in gq:
        g.first()

    for i in range(3, 8):
        x_loads[i].wait()
    norm_rows(3 * block, 6 * block)
    for g in gq:
        g.pass_on(0)
    norm_rows(6 * block, 8 * block)

    wo_load.wait()
    transpose = remote(wo_own, wo.at[partner["x"], partner["y"]], tp_s, tp_r, partner)
    stay = pltpu.make_async_copy(wo_own, wo.at[x, y], tp_r)

    @pl.when(s != h)
    def _():
        transpose.start()

    @pl.when(s == h)
    def _():
        stay.start()

    for g in gq:
        g.second()

    each_peer(lambda k: red_copy(k).wait_recv())
    total = part[0]
    for k in range(1, 16):
        total = total + red[k]
    key = total[:, :heads]
    eye = lax.broadcasted_iota(jnp.int32, (rows, 128), 0) == lax.broadcasted_iota(
        jnp.int32, (rows, 128), 1
    )
    key_sq = jnp.sum(key * key, axis=-1, keepdims=True)
    ssk_own[...] = jnp.sum(jnp.where(eye, key_sq, 0.0), axis=0, keepdims=True)

    def exchange(own, slots, send, recv):
        def copy(k):
            return remote(own, slots.at[k], send.at[k], recv.at[k], line(k))

        return copy

    sk_copy = exchange(ssk_own, ssk, sk_s, sk_r)
    each_peer(lambda k: sk_copy(k).start())
    for g in gq:
        g.pass_on(1)
        g.pass_on(2)
    kv[s, :, heads:] = total[:, heads:].astype(BF16)

    gcol[...] = jnp.broadcast_to(
        jnp.sum(jnp.where(diagonal(heads), qg_ref[...], 0.0), axis=1, keepdims=True), gcol.shape
    )
    xt[...] = xv[:, pl.ds(pl.multiple_of(z * (2 * depth), 128), 2 * depth)].T

    att_width = jnp.float32(16 * heads)
    each_peer(lambda k: sk_copy(k).wait_recv())
    sk_sum = ssk_own[...]
    for k in range(1, 16):
        sk_sum = sk_sum + ssk[k]
    key_rms = 1.0 / jnp.sqrt(sk_sum / att_width + 1e-06)
    key_scale = jnp.sum(jnp.where(eye, key_rms, 0.0), axis=-1, keepdims=True)
    kv[s, :, :heads] = (key * key_scale * kg_ref[...]).astype(BF16)

    def kv_copy(k):
        return remote(kv.at[s], kv.at[s], kv_s.at[k], kv_r.at[k], plane(k))

    def kv_wait(k):
        dev = plane(k, -1)
        src = dev["x"] * 4 + dev["y"]
        return remote(kv.at[src], kv.at[src], kv_s.at[k], kv_r.at[k], dev)

    each_peer(lambda k: kv_copy(k).start())
    for g in gq:
        g.pass_on(3)
    for g in gq:
        g.finish()

    for i in range(4):
        piece = jnp.dot(
            nv[:, i * 4 * depth : (i + 1) * 4 * depth],
            wq[i].reshape(4 * depth, heads),
            preferred_element_type=F32,
        )
        if i == 0:
            acc_q = piece
        else:
            acc_q = acc_q + piece
    qt[...] = acc_q.T
    ssq_own[...] = jnp.sum(qt[...] * qt[...], axis=0, keepdims=True)
    sq_copy = exchange(ssq_own, ssq, sq_s, sq_r)
    each_peer(lambda k: sq_copy(k).start())

    @pl.when(s != h)
    def _():
        transpose.wait_recv()
        transpose.wait_send()

    @pl.when(s == h)
    def _():
        stay.wait()

    go = [
        PlaneGather(wo, go_s.at[0], go_r.at[0], coords, "x", "y", 0, half),
        PlaneGather(wo, go_s.at[1], go_r.at[1], coords, "y", "x", half, half),
    ]
    for g in go:
        g.start()

    each_peer(lambda k: kv_wait(k).wait_recv())
    text = 16 * rows
    vt[...] = kv[:, :, heads:].reshape(text, heads).T

    each_peer(lambda k: sq_copy(k).wait_recv())
    sq_sum = ssq_own[...]
    for k in range(1, 16):
        sq_sum = sq_sum + ssq[k]
    query_rms = 1.0 / jnp.sqrt(sq_sum / att_width + 1e-06)

    valid = valid_ref[0]
    cols = 256

    def z_copy(flow, d, j, own):
        step = 1 if flow == 0 else 7
        back = (8 - d) if flow == 0 else d
        if own:
            back = (8 - d + 1) if flow == 0 else d - 1
        src = lax.rem(z + back, 8)
        ref = att.at[src, c, j]
        return remote(
            ref, ref, z_s.at[flow, d, j], z_r.at[flow, d, j], {"z": lax.rem(z + step, 8)}
        )

    def d_copy(flow, d, j, own):
        back = (8 - d) if flow == 0 else d
        src = lax.rem(z + back, 8)
        ref = att.at[src, c if own else 1 - c, j]
        return remote(ref, ref, d_s.at[flow, d, j], d_r.at[flow, d, j], {"c": 1 - c})

    for j in range(heads // HD):
        for t in range(tokens // cols):
            tok = slice(t * cols, (t + 1) * cols)
            hd = slice(j * HD, (j + 1) * HD)
            query = (
                qt[hd, tok] * query_rms[:, tok] * jnp.broadcast_to(gcol[hd, 0:1], (HD, cols))
            ).astype(BF16)
            keys = kv[:, :, hd].reshape(text, HD)
            scores = jnp.dot(keys, query, preferred_element_type=F32) * HD ** (-0.5)
            ok = lax.broadcasted_iota(jnp.int32, (text, cols), 0) < valid
            scores = jnp.where(ok, scores, -1e30)
            shifted = jnp.exp(scores - jnp.max(scores, axis=0, keepdims=True))
            weights = (shifted * (1.0 / jnp.sum(shifted, axis=0, keepdims=True))).astype(BF16)
            att[z, c, j, :, tok] = jnp.dot(
                vt[hd, :], weights, preferred_element_type=F32
            ).astype(BF16)
        z_copy(0, 1, j, True).start()
        z_copy(1, 1, j, True).start()
        d_copy(0, 0, j, True).start()
        if j == 0:
            for g in go:
                g.first()

    for g in go:
        g.pass_on(0)
    for g in go:
        g.second()
    for g in go:
        g.pass_on(1)
        g.pass_on(2)

    def project(zz, cc, first=False):
        src = zz * 2 + cc
        w = wo[lax.div(src, 4), lax.rem(src, 4)]
        term = jnp.dot(w, att[zz, cc].reshape(heads, tokens), preferred_element_type=F32)
        acc[...] = term if first else acc[...] + term

    def forward(d):
        for j in range(2):
            for flow in range(2):
                z_copy(flow, d, j, False).wait_recv()
                if d < 3 or j == flow:
                    z_copy(flow, d + 1, j, True).start()
                d_copy(flow, d, j, True).start()

    def add_in(d):
        for flow in range(2):
            zz = lax.rem(z + ((8 - d) if flow == 0 else d), 8)
            for j in range(2):
                d_copy(flow, d, j, False).wait_recv()
            project(zz, c)
            project(zz, 1 - c)

    forward(1)
    for g in go:
        g.pass_on(3)
    for g in go:
        g.finish()
    for j in range(2):
        d_copy(0, 0, j, False).wait_recv()
    project(z, c, True)
    project(z, 1 - c)
    forward(2)
    add_in(1)
    forward(3)
    add_in(2)
    add_in(3)
    far = lax.rem(z + 4, 8)
    for j in range(2):
        z_copy(j, 4, j, False).wait_recv()
        d_copy(j, 4, j, True).start()
    for j in range(2):
        d_copy(j, 4, j, False).wait_recv()
    project(far, c)
    project(far, 1 - c)

    resid = (xt[pl.ds(pl.multiple_of(c * depth, 16), depth), :].astype(F32) + acc[...]).astype(BF16)
    resid_ref[...] = resid
    wide = resid.astype(F32)
    st_own[0:1, :] = jnp.sum(wide, axis=0, keepdims=True)
    st_own[1:2, :] = jnp.sum(wide * wide, axis=0, keepdims=True)
    st_copy = exchange(st_own, st, st_s, st_r)
    each_peer(lambda k: st_copy(k).start())

    def drain(k):
        ctx_copy(k).wait_send()
        red_copy(k).wait_send()
        sk_copy(k).wait_send()
        kv_copy(k).wait_send()
        sq_copy(k).wait_send()

    each_peer(drain)
    for g in gq + go:
        g.wait_sends()
    for flow in range(2):
        for d in range(1, 5):
            for j in range(2):
                if d < 4 or j == flow:
                    z_copy(flow, d, j, True).wait_send()
                    d_copy(flow, d, j, True).wait_send()
    for j in range(2):
        d_copy(0, 0, j, True).wait_send()

    each_peer(lambda k: st_copy(k).wait_recv())
    stats = st_own[...]
    for k in range(1, 16):
        stats = stats + st[k]
    mean2 = stats[0:1, :] / width
    var2 = stats[1:2, :] / width - mean2 * mean2
    stat_ref[0:1, :] = mean2
    stat_ref[1:2, :] = 1.0 / jnp.sqrt(var2 + 1e-06)
    each_peer(lambda k: st_copy(k).wait_send())


def fused(valid_length, video, context, wq, wk, wv, wo_t, query_gain, key_gain):
    tokens, width = video.shape
    depth, heads = wq.shape
    rows = context.shape[0]
    pad = -(-depth // 128) * 128
    dma = pltpu.SemaphoreType.DMA
    any_spec = pl.BlockSpec(memory_space=pl.ANY)
    vmem = pl.BlockSpec(memory_space=pltpu.VMEM)
    return pl.pallas_call(
        kernel,
        out_shape=(
            jax.ShapeDtypeStruct((depth, tokens), BF16),
            jax.ShapeDtypeStruct((2, tokens), F32),
        ),
        in_specs=[pl.BlockSpec(memory_space=pltpu.SMEM)] + [any_spec] * 6 + [vmem] * 2,
        out_specs=(vmem, vmem),
        scratch_shapes=[
            pltpu.VMEM((tokens, width), BF16),
            pltpu.VMEM((tokens, width), BF16),
            pltpu.VMEM((4, 4, depth, heads), BF16),
            pltpu.VMEM((4, 4, depth, heads), BF16),
            pltpu.VMEM((depth, heads), BF16),
            pltpu.VMEM((rows, width), BF16),
            pltpu.VMEM((16, rows, pad), BF16),
            pltpu.VMEM((16, rows, pad), BF16),
            pltpu.VMEM((pad, 2 * heads), BF16),
            pltpu.VMEM((16, rows, 2 * heads), F32),
            pltpu.VMEM((16, rows, 2 * heads), F32),
            pltpu.VMEM((16, rows, 2 * heads), BF16),
            pltpu.VMEM((heads, 16 * rows), BF16),
            pltpu.VMEM((heads, tokens), F32),
            pltpu.VMEM((8, 2, heads // HD, HD, tokens), BF16),
            pltpu.VMEM((depth, tokens), F32),
            pltpu.VMEM((2 * depth, tokens), BF16),
            pltpu.VMEM((heads, 128), F32),
            pltpu.VMEM((1, 128), F32),
            pltpu.VMEM((16, 1, 128), F32),
            pltpu.VMEM((1, tokens), F32),
            pltpu.VMEM((16, 1, tokens), F32),
            pltpu.VMEM((2, tokens), F32),
            pltpu.VMEM((16, 2, tokens), F32),
            dma((13,)),
            dma((2, 20)), dma((2, 20)), dma((2, 20)), dma((2, 20)),
            dma, dma,
            dma((16,)), dma((16,)), dma((16,)), dma((16,)), dma((16,)), dma((16,)),
            dma((16,)), dma((16,)), dma((16,)), dma((16,)), dma((16,)), dma((16,)),
            dma((2, 5, 2)), dma((2, 5, 2)), dma((2, 5, 2)), dma((2, 5, 2)),
        ],
        compiler_params=pltpu.CompilerParams(
            collective_id=0, has_side_effects=True, vmem_limit_bytes=60 * 1024 * 1024
        ),
        name="cross",
    )(valid_length, video, context, wq, wk, wv, wo_t, query_gain[None, :], key_gain[None, :])


def on_device(
    video_rows,
    context,
    valid_length,
    timestep,
    query_weight,
    key_weight,
    value_weight,
    out_weight,
    query_gain,
    key_gain,
    time_weight,
    modulation,
):
    resid_t, stats = fused(
        valid_length, video_rows, context, query_weight, key_weight, value_weight, out_weight.T,
        query_gain, key_gain,
    )
    half = FREQ // 2
    freqs = jnp.exp(-jnp.log(10000.0) * jnp.arange(half, dtype=F32) / half)
    angles = timestep[0].astype(F32) * freqs
    embedding = jnp.concatenate([jnp.cos(angles), jnp.sin(angles)])
    act = jax.nn.silu(embedding).astype(BF16)[None, :]
    shift = modulation[0] + jnp.dot(act, time_weight[0], preferred_element_type=F32)[0]
    scale = modulation[1] + jnp.dot(act, time_weight[1], preferred_element_type=F32)[0]
    resid = resid_t.astype(F32)
    modulated = (
        (resid - stats[0:1]) * stats[1:2] * (1.0 + scale)[:, None] + shift[:, None]
    ).astype(BF16)
    return resid_t.T, modulated.T


def solution(mesh):
    split = Mesh(mesh.devices.reshape(4, 4, 8, 2), ("x", "y", "z", "c"))
    line = ("z", "c")
    return jax.shard_map(
        on_device,
        mesh=split,
        in_specs=(
            P(SEQ, None),
            P(SEQ, None),
            P(),
            P(),
            P(SEQ, line),
            P(SEQ, line),
            P(SEQ, line),
            P(line, SEQ),
            P(line),
            P(line),
            P(None, None, line),
            P(None, line),
        ),
        out_specs=(P(SEQ, line), P(SEQ, line)),
        check_vma=False,
    )
```

time: 245 us -> 119 us (0.49)
  Pallas kernels: 0 us -> 109 us
  waiting for transfers between devices: 106 us -> 0 us
  blocking collectives: 62.8 us -> 0 us
  starting transfers between devices: 24.1 us -> 0 us
  matrix products: 18.7 us -> 2.22 us
  between operations: 15.3 us -> 1.98 us
  other arithmetic: 11.6 us -> 1.93 us
  local copies, waits for them, and re-layouts: 5.73 us -> 3.26 us
    pallas_call x0 -> x1, Pallas kernels: none -> 109 us  [fused(): pl.pallas_call(kernel, out_shape=(jax.ShapeDtypeStruct((depth, tokens), B...]
    reduce_scatter x1 -> x0, waiting for transfers between devices: 68.9 us -> none  [on_device(): projected = lax.psum_scatter(terms, 'head', scatter_dimension=1, tiled=True)]
    all_gather x2 -> x0, blocking collectives: 62.8 us -> none  [the longest x1 40.4 us: gathered_by_axis(): nearer = lax.all_gather(shard, axes[-1], axis=dim, tiled=True)]
    all_gather x2 -> x0, waiting for transfers between devices: 24.8 us -> none  [the longest x1 24.8 us: side_by_side(): lax.all_gather(both, axis, axis=dim, tiled=True)]
    all_to_all x3 -> x0, starting transfers between devices: 24 us -> none  [from_everyone(): return lax.all_to_all(copies, axis, split_axis=0, concat_axis=0, tiled=True)]
    dot_general x7 -> x2, matrix products: 17.9 us -> 2.22 us  [the longest x1 1.11 us: on_device(): jnp.dot(act, time_weight[0], preferred_element_type=F32)[0]]
    all_to_all x3 -> x0, waiting for transfers between devices: 12.4 us -> none  [from_everyone(): return lax.all_to_all(copies, axis, split_axis=0, concat_axis=0, tiled=True)]
    reduce_sum x5 -> x0, other arithmetic: 8.57 us -> none  [the longest x1 3.99 us: layer_norm(): spread = jnp.mean((rows - mean) ** 2, axis=-1, keepdims=True)]
  transfers between devices with their start and end apart: 6 -> 0, of which waited for: 4 -> 0; matrix products, arithmetic and copies ran while one was open for 10% -> 0% of each run, Pallas kernels for 0% -> 0%
where the time goes in v1:
time: 119 us
  Pallas kernels  109 us (92%)
  local copies, waits for them, and re-layouts  3.26 us (3%)
  matrix products  2.22 us (2%)
  between operations  1.98 us (2%)
  other arithmetic  1.93 us (2%)
    pallas_call x1, Pallas kernels, fused(): pl.pallas_call(kernel, out_shape=(jax.ShapeDtypeStruct((depth, tokens), B...  109 us

profile of v1, /device:TPU:1, one launch (start us, length us, event | category | flops | bytes accessed | tf_op | source)
XLA Modules:
  0.0 118.8 jit_solution(9874778035756821915)
XLA Ops:
  2.0 1.1 convolution_reduce_fusion
  3.1 1.1 convolution_reduce_fusion.1
  4.2 0.8 slice_reduce_fusion.1
  5.0 109.4 %cross.1 = (bf16[320,512]{1,0:T(8,128)(2,1)}, f32[2,512]{1,0:T(2,128)}) custom-call(s32[1]{0:T(128)S(6)} %copy.15.valid_ref, bf16[512,5120]{1,0:T(8,128)(2,1)} %x_hbm.1, bf16[32,5120]{1,0:T(8,128)(2,1)} %ctx_hbm.1, bf16[320,256]{1,0:T(8,128)(2,1)} %wq_hbm.1, bf16[320,256]{1,0:T(8,128)(2,1)} %wk_hbm.1, bf16[320,256]{1,0:T(8,128)(2,1)} %wv_hbm.1, ...), custom_call_target="tpu_custom_call" | custom-call | tf_op jit(solution)/shard_map/cross/pallas_call | solution.py:483
  114.5 0.8 fusion.8
  115.2 1.9 %fusion = bf16[512,320]{0,1:T(8,128)(2,1)} fusion(bf16[320,512]{1,0:T(8,128)(2,1)} %get-tuple-element.4, f32[320]{0:T(512)S(1)} %add.37, f32[320]{0:T(512)S(1)} %add_add_fusion, f32[512]{0:T(512)S(1)} %bitcast.20, f32[512]{0:T(512)S(1)} %bitcast.19), kind=kLoop, calls=%fused_computation.3 | loop fusion | flops 983040 | bytes 662016 | tf_op jit(solution)/shard_map/transpose | solution.py:559
  117.1 1.7 %copy.17 = bf16[512,320]{0,1:T(8,128)(2,1)} copy(bf16[512,320]{0,1:T(8,128)(2,1)} %bitcast.17) | data formatting | bytes 655360
  (5 shorter events, 0.1 us)
